TPU v7x, 128 devices: a whole 4x4x4 slice. The times are simulated.
128 devices in a mesh: lat: 8 (over x, core), lon: 16 (over y, z).
Axes of the slice: x: 4, y: 4, z: 4, core: 2. Of those that a mesh axis runs over, the one named last changes fastest.
Arguments:
- spectra: bfloat16 [393216, 616], P(('lat', 'lon')), may hold values from -6 to 6
- block_target: int32 [3072], P(('lat', 'lon')), may hold values from 0 to 15, as said below
- block_patch: int32 [3072], P(('lat', 'lon')), may hold values from 0 to 11
- block_kernel: int32 [3072], P(('lat', 'lon')), may hold values from 0 to 15
- encoder_weight: bfloat16 [616, 512], replicated, may hold values from -0.25 to 0.25
- kernels: bfloat16 [16, 128, 128], replicated, may hold values from 0.049804688 to 1
- gain: float32 [512], replicated, may hold values from 0.1 to 1.9
- conv_weight: bfloat16 [3, 3, 512, 512], replicated, may hold values from -0.09375 to 0.09375
- cotangent: bfloat16 [192, 1024, 512], P('lat', 'lon'), may hold values from -6 to 6
Outputs:
- conv_out: bfloat16 [192, 1024, 512], P('lat', 'lon')
- conv_grad: float32 [3, 3, 512, 512], replicated
- encoder_grad: float32 [616, 512], replicated
- gain_grad: float32 [512], replicated
Inputs may be any that keep to these rules, and one draw needn't show every extreme that they name: `block_target`: within one device's 24 blocks no tile is named more than 3 times; in every latitude band one tile is named exactly 3 times by every device of the band.
All inputs are finite; a program needn't handle non-finite values.
Results may differ from a plain program's by a relative error of at most 0.0059.
Values may be sent and summed in bfloat16 or wider, within the bound.
A program may use at most 192 MiB of HBM per device.

v0:
```python
import math
import jax
import jax.numpy as jnp
from jax import lax
from jax.sharding import PartitionSpec as P

PH = 8
PW = 16
MOST = 3


def padded_2(shard, sides, width, wrap):
    for axis, dim in sides:
        size, length = (lax.axis_size(axis), shard.shape[dim])
        up = [(i, (i + 1) % size) for i in range(size if wrap else size - 1)]
        down = [(j, i) for i, j in up]
        last = lax.slice_in_dim(shard, length - width, length, axis=dim)
        leading = lax.slice_in_dim(shard, 0, width, axis=dim)
        before = lax.ppermute(last, axis, up)
        after = lax.ppermute(leading, axis, down)
        shard = jnp.concatenate([before, shard, after], axis=dim)
    return shard


def gather_turned(arrays, axis, dims):
    turned = [jnp.moveaxis(a, dim, 0) for a, dim in zip(arrays, dims)]
    both = jnp.concatenate([t.reshape(len(t), -1) for t in turned], axis=1)
    result, at, finished = (lax.all_gather(both, axis, axis=0, tiled=True), 0, [])
    for t, dim in zip(turned, dims):
        piece = result[:, at : at + t[0].size].reshape(-1, *t.shape[1:])
        finished.append(jnp.moveaxis(piece, 0, dim))
        at += t[0].size
    return tuple(finished)


def normalise(field, gain):
    meansq = jnp.mean(field * field, axis=-1, keepdims=True)
    return field * lax.rsqrt(meansq + 1e-06) * gain


def silu_slope(preact):
    logistic = jax.nn.sigmoid(preact)
    return logistic * (1.0 + preact * (1.0 - logistic))


def widen(field):
    beside_all = padded_2(field, (("lon", 1),), 1, True)
    return padded_2(beside_all, (("lat", 0),), 1, False)


def slot_layout(targets, lon_count):
    lanes = jnp.arange(lon_count, dtype=jnp.int32)
    onehot = (targets[..., None] == lanes).astype(jnp.int32)
    before = jnp.cumsum(onehot, axis=-2) - onehot
    ranks = jnp.sum(before * onehot, axis=-1)
    return targets * MOST + ranks


def to_tile(patches_in, tile_rows, tile_cols, width):
    shaped = patches_in.reshape(tile_rows // PH, tile_cols // PW, PH, PW, width)
    return shaped.transpose(0, 2, 1, 3, 4).reshape(tile_rows, tile_cols, width)


def to_patches(tile, tile_rows, tile_cols, width):
    shaped = tile.reshape(tile_rows // PH, PH, tile_cols // PW, PW, width)
    return shaped.transpose(0, 2, 1, 3, 4).reshape(-1, PH * PW, width)


def shards(
    spectra,
    block_target,
    block_patch,
    block_kernel,
    encoder_weight,
    kernels,
    gain,
    conv_weight,
    cotangent,
):
    lon_count = lax.axis_size("lon")
    lat_count = lax.axis_size("lat")
    own_lon = lax.axis_index("lon")
    blocks = block_target.shape[0]
    kernel_count, block_rows, patch_cells = kernels.shape
    channels = spectra.shape[1]
    width = encoder_weight.shape[1]
    tile_rows, tile_cols = (cotangent.shape[0], cotangent.shape[1])
    slots = lon_count * MOST
    patch_count = tile_rows // PH * (tile_cols // PW)
    loss_scale = 1.0 / math.sqrt(tile_rows * lat_count * tile_cols * lon_count)
    all_target, all_patch, all_kernel = gather_turned(
        (block_target, block_patch, block_kernel), "lon", (0, 0, 0)
    )
    all_target = all_target.reshape(lon_count, blocks)
    all_patch = all_patch.reshape(lon_count, blocks)
    all_kernel = all_kernel.reshape(lon_count, blocks)
    own_slot = slot_layout(block_target, lon_count)
    slot_ids = jnp.arange(slots, dtype=jnp.int32)
    chosen_slots = own_slot[None, :] == slot_ids[:, None]
    filled = jnp.any(chosen_slots, axis=1)
    source_block = jnp.sum(chosen_slots * jnp.arange(blocks, dtype=jnp.int32)[None, :], axis=1)
    all_slot = slot_layout(all_target, lon_count)
    wanted = own_lon * MOST + jnp.arange(MOST, dtype=jnp.int32)
    arrive = (all_slot[:, None, :] == wanted[None, :, None]).astype(jnp.int32)
    present = jnp.sum(arrive, axis=2).reshape(-1) > 0
    slot_kernel = jnp.sum(arrive * all_kernel[:, None, :], axis=2).reshape(-1)
    slot_kernel = jnp.where(present, slot_kernel, -1)
    slot_patch = jnp.sum(arrive * all_patch[:, None, :], axis=2).reshape(-1)
    taken = jnp.take(spectra.reshape(blocks, block_rows, channels), source_block, axis=0)
    taken = jnp.where(filled[:, None, None], taken, jnp.zeros_like(taken))
    arrived = lax.all_to_all(
        taken.reshape(lon_count, MOST, -1), "lon", split_axis=0, concat_axis=0, tiled=True
    )
    slot_spectra = arrived.reshape(slots * block_rows, channels)
    slot_preact = jnp.dot(slot_spectra, encoder_weight, preferred_element_type=jnp.float32)
    slot_rows = jax.nn.silu(slot_preact).astype(jnp.bfloat16).reshape(slots, block_rows, width)
    kernel_pick = (
        slot_kernel[:, None] == jnp.arange(kernel_count, dtype=jnp.int32)[None, :]
    ).astype(jnp.bfloat16)
    slot_kernels = jnp.dot(
        kernel_pick, kernels.reshape(kernel_count, -1), preferred_element_type=jnp.float32
    )
    slot_kernels = slot_kernels.astype(jnp.bfloat16).reshape(slots, block_rows, patch_cells)
    contribution = jnp.einsum(
        "sbp,sbd->spd", slot_kernels, slot_rows, preferred_element_type=jnp.float32
    )
    patch_pick = (slot_patch[:, None] == jnp.arange(patch_count, dtype=jnp.int32)[None, :]).astype(
        jnp.float32
    )
    tile_patches = jnp.einsum(
        "sq,spd->qpd", patch_pick, contribution, precision=lax.Precision.HIGHEST
    )
    spread = to_tile(tile_patches, tile_rows, tile_cols, width)
    normed = normalise(spread, gain).astype(jnp.bfloat16)
    padded = widen(normed)
    windows = []
    result_sum = jnp.zeros((tile_rows * tile_cols, width), jnp.float32)
    for row_shift in range(3):
        for col_shift in range(3):
            window = padded[
                row_shift : row_shift + tile_rows, col_shift : col_shift + tile_cols
            ].reshape(-1, width)
            windows.append(window)
            result_sum = result_sum + jnp.dot(
                window, conv_weight[row_shift, col_shift], preferred_element_type=jnp.float32
            )
    conv_out = result_sum.reshape(tile_rows, tile_cols, width).astype(jnp.bfloat16)
    cot_padded = widen(cotangent)
    cot_flat = cotangent.reshape(-1, width)
    d_normed = jnp.zeros((tile_rows * tile_cols, width), jnp.float32)
    kernel_grads = []
    for row_shift in range(3):
        for col_shift in range(3):
            back_window = cot_padded[
                2 - row_shift : 2 - row_shift + tile_rows, 2 - col_shift : 2 - col_shift + tile_cols
            ].reshape(-1, width)
            d_normed = d_normed + lax.dot_general(
                back_window,
                conv_weight[row_shift, col_shift],
                (((1,), (1,)), ((), ())),
                preferred_element_type=jnp.float32,
            )
            kernel_grads.append(
                lax.dot_general(
                    windows[row_shift * 3 + col_shift],
                    cot_flat,
                    (((0,), (0,)), ((), ())),
                    preferred_element_type=jnp.float32,
                )
            )
    conv_part = jnp.stack(kernel_grads).reshape(3, 3, width, width)
    _, pullback = jax.vjp(normalise, spread, gain)
    d_spread, gain_part = pullback(d_normed.reshape(tile_rows, tile_cols, width))
    d_patches = to_patches(d_spread.astype(jnp.bfloat16), tile_rows, tile_cols, width)
    slot_dpatch = jnp.take(d_patches, slot_patch, axis=0)
    slot_drows = jnp.einsum(
        "sbp,spd->sbd", slot_kernels, slot_dpatch, preferred_element_type=jnp.float32
    ).astype(jnp.bfloat16)
    d_preact = (slot_drows.reshape(-1, width).astype(jnp.float32) * silu_slope(slot_preact)).astype(
        jnp.bfloat16
    )
    encoder_part = lax.dot_general(
        slot_spectra, d_preact, (((0,), (0,)), ((), ())), preferred_element_type=jnp.float32
    )
    conv_total, encoder_total, gain_total = lax.psum(
        (conv_part, encoder_part, gain_part), ("lat", "lon")
    )
    return (conv_out, conv_total * loss_scale, encoder_total * loss_scale, gain_total * loss_scale)


def solution(mesh):
    placed = (
        P(("lat", "lon"), None),
        P(("lat", "lon")),
        P(("lat", "lon")),
        P(("lat", "lon")),
        P(),
        P(),
        P(),
        P(),
        P("lat", "lon", None),
    )
    return jax.shard_map(
        shards,
        mesh=mesh,
        in_specs=placed,
        out_specs=(P("lat", "lon", None), P(), P(), P()),
        check_vma=False,
    )
```

profile of v0, /device:TPU:1, one launch (start us, length us, event | category | flops | bytes accessed | tf_op | source)
XLA Modules:
  0.0 534.1 jit_solution(6251264387614628848)
XLA Ops:
  10.5 20.2 %all-gather = s32[16,24,3]{1,2,0:T(4,128)S(1)} all-gather(s32[1,24,3]{1,2,0:T(4,128)S(1)} %add_bitcast_fusion), channel_id=1, replica_groups=mesh['lat'=8,'lon'=16] {'lon'}, dimensions={0}, use_global_device_ids=true | all-gather | bytes 4896 | tf_op jit(solution)/shard_map/all_gather | solution.py:28
  32.4 4.6 copy_bitcast_fusion
  37.0 7.6 %gather_fusion = bf16[48,128,616]{1,2,0:T(8,128)(2,1)} fusion(bf16[24,128,616]{1,2,0:T(8,128)(2,1)} %copy_bitcast_fusion, s32[1024]{0:T(1024)S(1)} %get-tuple-element.49), kind=kCustom, calls=%fused_computation | custom fusion | bytes 15139008 | tf_op jit(solution)/shard_map/jit(_take)/gather | solution.py:109
  44.6 10.3 %copy.102 = bf16[48,128,616]{2,1,0:T(8,128)(2,1)} copy(bf16[48,128,616]{1,2,0:T(8,128)(2,1)} %gather_fusion) | data formatting | bytes 15138816 | tf_op jit(solution)/shard_map/jit(_take)/gather | solution.py:109
  54.9 20.1 %gather.11 = bf16[16,3,78848]{2,1,0:T(4,128)(2,1)} reshape(bf16[48,128,616]{2,1,0:T(8,128)(2,1)} %copy.102) | data formatting | bytes 15138816 | tf_op jit(solution)/shard_map/jit(_take)/gather | solution.py:109
  75.3 9.7 %select_select_fusion = bf16[16,3,78848]{2,1,0:T(4,128)(2,1)} fusion(bf16[16,3,78848]{2,1,0:T(4,128)(2,1)} %gather.11, pred[16,3]{1,0:T(8,128)(4,1)S(1)} %copy.100, pred[16,3]{1,0:T(8,128)(4,1)S(1)} %broadcast_in_dim.57), kind=kLoop, calls=%fused_computation.9 | loop fusion | flops 7569408 | bytes 15138912 | tf_op jit(solution)/shard_map/jit(_where)/select_n | solution.py:110
  85.0 5.0 all-to-all-start
  90.2 1.4 collective-permute-start.4
  91.5 3.5 collective-permute-start.5
  95.3 2.1 fusion.41
  98.1 1.6 copy.116
  99.6 104.8 %collective-permute-done.4 = bf16[24,1,512]{2,1,0:T(2,128)(2,1)S(1)} collective-permute-done((bf16[24,1,512]{2,1,0:T(2,128)(2,1)S(1)}, bf16[24,1,512]{2,1,0:T(2,128)(2,1)S(1)}, u32[]{:S(2)}, u32[]{:S(2)}) %collective-permute-start.4) | collective-permute-done | bytes 24608 | tf_op jit(solution)/shard_map/ppermute | solution.py:19
  204.5 5.4 %collective-permute-done.5 = bf16[24,1,512]{2,1,0:T(2,128)(2,1)S(1)} collective-permute-done((bf16[24,1,512]{2,1,0:T(2,128)(2,1)S(1)}, bf16[24,1,512]{2,1,0:T(2,128)(2,1)S(1)}, u32[]{:S(2)}, u32[]{:S(2)}) %collective-permute-start.5) | collective-permute-done | bytes 24608 | tf_op jit(solution)/shard_map/ppermute | solution.py:20
  210.0 8.4 %collective-permute-start.6 = (bf16[1,66,512]{2,1,0:T(8,128)(2,1)S(1)}, bf16[1,66,512]{2,1,0:T(8,128)(2,1)S(1)}, u32[]{:S(2)}, u32[]{:S(2)}) collective-permute-start(bf16[1,66,512]{2,1,0:T(8,128)(2,1)S(1)} %get-tuple-element.34), channel_id=1, source_target_pairs={{16,0},{32,16},{48,32},{64,48},{80,64},{96,80},{112,96},{17,1},{33... | collective-permute-start | bytes 202760 | tf_op jit(solution)/shard_map/ppermute | solution.py:20
  218.4 3.2 collective-permute-start.7
  221.6 1.1 pad_maximum_fusion.2
  222.8 2.0 pad_maximum_fusion.1
  224.8 2.3 fusion.96
  227.2 1.0 fusion.49
  228.3 1.0 fusion.35
  229.3 1.1 convolution_add_fusion.5
  230.4 1.0 convolution_add_fusion.4
  231.4 1.1 fusion.10
  232.5 1.1 fusion.9
  233.6 1.0 convolution_add_fusion.1
  234.7 2.7 convolution_add_fusion
  237.4 20.1 %reshape.267 = bf16[6144,616]{1,0:T(8,128)(2,1)} reshape(bf16[16,3,78848]{2,1,0:T(4,128)(2,1)} %all-to-all-done) | data formatting | bytes 15138816 | tf_op jit(solution)/shard_map/reshape | solution.py:114
  257.5 11.7 %multiply_convert_fusion = (bf16[6144,512]{1,0:T(8,128)(2,1)S(1)}, f32[6144,512]{1,0:T(8,128)}) fusion(bf16[6144,616]{1,0:T(8,128)(2,1)} %reshape.267, bf16[616,512]{1,0:T(8,128)(2,1)S(1)} %copy-done), kind=kOutput, calls=%fused_computation.7 | convolution fusion | flops 3891265536 | bytes 27074560 | tf_op jit(solution)/shard_map/dot_general | solution.py:115
  269.2 1.8 fusion.101
  271.1 12.0 %fusion.1 = f32[12,128,512]{2,0,1:T(8,128)S(1)} fusion(f32[48,128,512]{2,1,0:T(8,128)S(1)} %fusion.101, s32[48]{0:T(128)S(1)} %eq.86), kind=kOutput, calls=%fused_computation.5 | convolution fusion | flops 452985408 | bytes 15728832 | tf_op jit(solution)/shard_map/sq,spd->qpd/dot_general | solution.py:130
  283.1 1.8 copy.105
  284.9 2.0 copy.106
  286.9 1.0 copy-done.3
  288.6 2.2 fusion.13
  290.8 2.2 multiply_convert_fusion.2
  293.1 1.2 copy-done.5
  294.4 4.8 collective-permute-start.1
  299.2 6.6 %gather_fusion.1 = bf16[48,128,512]{2,1,0:T(8,128)(2,1)} fusion(bf16[12,128,512]{2,1,0:T(8,128)(2,1)} %bitcast.199, s32[1024]{0:T(1024)S(1)} %get-tuple-element.48), kind=kCustom, calls=%fused_computation.1 | custom fusion | bytes 12583104 | tf_op jit(solution)/shard_map/jit(_take)/gather | solution.py:175
  305.7 5.3 fusion.6
  311.0 7.8 %fusion = bf16[6144,512]{1,0:T(8,128)(2,1)S(1)} fusion(f32[6144,512]{1,0:T(8,128)} %get-tuple-element.47, bf16[48,128,512]{2,1,0:T(8,128)(2,1)S(1)} %fusion.6), kind=kLoop, calls=%fused_computation.4 | loop fusion | flops 31457280 | bytes 25165824 | tf_op jit(solution)/shard_map/convert_element_type | solution.py:179
  318.8 5.1 fusion.102
  324.0 4.8 collective-permute-start.2
  328.9 1.9 collective-permute-start.3
  330.8 1.1 pad_maximum_fusion.4
  332.0 2.6 collective-permute-done.3
  334.5 2.3 maximum_maximum_fusion
  337.9 1.0 fusion.26
  338.9 1.0 fusion.25
  344.0 1.0 fusion.20
  345.0 1.0 fusion.19
  346.1 3.7 copy-done.16
  350.0 2.9 copy.108
  352.8 2.3 fusion.15
  355.1 66.0 %psum.23 = f32[512]{0:T(512)S(1)} all-reduce(f32[512]{0:T(512)S(1)} %fusion.15), channel_id=1, replica_groups=mesh['lat'=8,'lon'=16] {'lat','lon'}, use_global_device_ids=true, to_apply=%region_14.15 | all-reduce | flops 512 | bytes 4096 | tf_op jit(solution)/shard_map/psum | solution.py:185
  421.7 2.6 fusion.43
  424.4 1.1 fusion.95
  427.1 1.1 fusion.94
  429.2 1.1 convolution_add_fusion.11
  430.3 1.1 convolution_add_fusion.10
  431.7 1.1 fusion.12
  435.1 2.2 fusion.17
  437.2 79.2 %all-reduce.3.cloned.1.call-done = (f32[3,3,512,512]{3,2,1,0:T(8,128)}, f32[616,512]{1,0:T(8,128)}) async-done(((f32[3,3,512,512]{3,2,1,0:T(8,128)}, f32[616,512]{1,0:T(8,128)}), (f32[3,3,512,512]{3,2,1,0:T(8,128)}, f32[616,512]{1,0:T(8,128)})) %all-reduce.3.cloned.1.call-update) | async-done | bytes 10698768 | tf_op jit(solution)/shard_map/psum | solution.py:185
  516.4 9.2 %broadcast_multiply_fusion = f32[3,3,512,512]{3,2,1,0:T(8,128)} fusion(f32[3,3,512,512]{3,2,1,0:T(8,128)} %get-tuple-element.12), kind=kLoop, calls=%fused_computation.14 | loop fusion | flops 2359296 | bytes 18874368 | tf_op jit(solution)/shard_map/mul | solution.py:188
  525.6 1.2 broadcast_multiply_fusion.1
  (115 shorter events, 18.4 us)
Async XLA Ops:
  7.2 250.3 %copy-start = (bf16[616,512]{1,0:T(8,128)(2,1)S(1)}, bf16[616,512]{1,0:T(8,128)(2,1)}, u32[]{:S(2)}) copy-start(bf16[616,512]{1,0:T(8,128)(2,1)} %param.13) | copy-start | bytes 1892356
  85.0 5.0 copy-start.2
  85.0 152.4 %all-to-all-start = ((bf16[16,3,78848]{2,1,0:T(4,128)(2,1)}), bf16[16,3,78848]{2,1,0:T(4,128)(2,1)}, u32[]{:S(2)}, u32[]{:S(2)}) async-start(bf16[16,3,78848]{2,1,0:T(4,128)(2,1)} %select_select_fusion), calls=%async_computation | async-start | bytes 20185088 | tf_op jit(solution)/shard_map/all_to_all | solution.py:111
  90.0 426.4 %all-reduce.3.cloned.1.call-start = ((), (), s32[]{:S(2)}) async-start(), calls=%async_computation.1 | async-start | bytes 21397504 | tf_op jit(solution)/shard_map/psum | solution.py:185
  90.2 114.3 %collective-permute-start.4 = (bf16[24,1,512]{2,1,0:T(2,128)(2,1)S(1)}, bf16[24,1,512]{2,1,0:T(2,128)(2,1)S(1)}, u32[]{:S(2)}, u32[]{:S(2)}) collective-permute-start(bf16[24,1,512]{2,1,0:T(2,128)(2,1)S(1)} %get-tuple-element.42), channel_id=1, source_target_pairs={{0,1},{1,2},{2,3},{3,4},{4,5},{5,6},{6,7},{7,8},{8,9},{9,10},{10,1... | collective-permute-start | bytes 73736 | tf_op jit(solution)/shard_map/ppermute | solution.py:19
  91.5 118.4 %collective-permute-start.5 = (bf16[24,1,512]{2,1,0:T(2,128)(2,1)S(1)}, bf16[24,1,512]{2,1,0:T(2,128)(2,1)S(1)}, u32[]{:S(2)}, u32[]{:S(2)}) collective-permute-start(bf16[24,1,512]{2,1,0:T(2,128)(2,1)S(1)} %get-tuple-element.43), channel_id=1, source_target_pairs={{1,0},{2,1},{3,2},{4,3},{5,4},{6,5},{7,6},{8,7},{9,8},{10,9},{11,1... | collective-permute-start | bytes 73736 | tf_op jit(solution)/shard_map/ppermute | solution.py:20
  95.3 2.2 copy-start.18
  210.0 12.7 %collective-permute-start.6 = (bf16[1,66,512]{2,1,0:T(8,128)(2,1)S(1)}, bf16[1,66,512]{2,1,0:T(8,128)(2,1)S(1)}, u32[]{:S(2)}, u32[]{:S(2)}) collective-permute-start(bf16[1,66,512]{2,1,0:T(8,128)(2,1)S(1)} %get-tuple-element.34), channel_id=1, source_target_pairs={{16,0},{32,16},{48,32},{64,48},{80,64},{96,80},{112,96},{17,1},{33... | collective-permute-start | bytes 202760 | tf_op jit(solution)/shard_map/ppermute | solution.py:20
  218.4 4.4 collective-permute-start.7
  222.8 4.4 slice-start
  224.8 2.4 slice-start.1
  257.5 11.7 %copy-start.9 = (bf16[6,8,128,128]{3,2,1,0:T(8,128)(2,1)S(1)}, bf16[6,8,128,128]{3,2,1,0:T(8,128)(2,1)}, u32[]{:S(2)}) copy-start(bf16[6,8,128,128]{3,2,1,0:T(8,128)(2,1)} %copy.116) | copy-start | bytes 4718596
  284.9 3.0 copy-start.3
  284.9 3.0 copy-start.19
  293.1 1.2 copy-start.5
  294.3 29.6 %collective-permute-start = (bf16[24,1,512]{2,1,0:T(2,128)(2,1)S(1)}, bf16[24,1,512]{2,1,0:T(2,128)(2,1)S(1)}, u32[]{:S(2)}, u32[]{:S(2)}) collective-permute-start(bf16[24,1,512]{2,1,0:T(2,128)(2,1)S(1)} %get-tuple-element.38), channel_id=1, source_target_pairs={{0,1},{1,2},{2,3},{3,4},{4,5},{5,6},{6,7},{7,8},{8,9},{9,10},{10,1... | collective-permute-start | bytes 73736 | tf_op jit(solution)/shard_map/ppermute | solution.py:19
  294.4 29.6 %collective-permute-start.1 = (bf16[24,1,512]{2,1,0:T(2,128)(2,1)S(1)}, bf16[24,1,512]{2,1,0:T(2,128)(2,1)S(1)}, u32[]{:S(2)}, u32[]{:S(2)}) collective-permute-start(bf16[24,1,512]{2,1,0:T(2,128)(2,1)S(1)} %get-tuple-element.39), channel_id=1, source_target_pairs={{1,0},{2,1},{3,2},{4,3},{5,4},{6,5},{7,6},{8,7},{9,8},{10,9},{11,1... | collective-permute-start | bytes 73736 | tf_op jit(solution)/shard_map/ppermute | solution.py:20
  305.7 13.0 %slice-start.4 = ((s8[7864320]{0:T(1024)(128)(4,1)}), s8[4194304]{0:T(1024)(128)(4,1)S(1)}, s32[]{:S(2)}) async-start(s8[7864320]{0:T(1024)(128)(4,1)} %bitcast.216), calls=%async_computation.6 | async-start | bytes 8388608
  311.0 7.8 %slice-start.5 = ((s8[7864320]{0:T(1024)(128)(4,1)}), s8[3670016]{0:T(1024)(128)(4,1)S(1)}, s32[]{:S(2)}) async-start(s8[7864320]{0:T(1024)(128)(4,1)} %bitcast.216), calls=%async_computation.7 | async-start | bytes 7340032
  318.8 5.2 copy-start.6
  324.0 7.9 %collective-permute-start.2 = (bf16[1,66,512]{2,1,0:T(8,128)(2,1)S(1)}, bf16[1,66,512]{2,1,0:T(8,128)(2,1)S(1)}, u32[]{:S(2)}, u32[]{:S(2)}) collective-permute-start(bf16[1,66,512]{2,1,0:T(8,128)(2,1)S(1)} %get-tuple-element.30), channel_id=1, source_target_pairs={{0,16},{16,32},{32,48},{48,64},{64,80},{80,96},{96,112},{1,17},{17... | collective-permute-start | bytes 202760 | tf_op jit(solution)/shard_map/ppermute | solution.py:19
  328.9 5.7 %collective-permute-start.3 = (bf16[1,66,512]{2,1,0:T(8,128)(2,1)S(1)}, bf16[1,66,512]{2,1,0:T(8,128)(2,1)S(1)}, u32[]{:S(2)}, u32[]{:S(2)}) collective-permute-start(bf16[1,66,512]{2,1,0:T(8,128)(2,1)S(1)} %get-tuple-element.31), channel_id=1, source_target_pairs={{16,0},{32,16},{48,32},{64,48},{80,64},{96,80},{112,96},{17,1},{33... | collective-permute-start | bytes 202760 | tf_op jit(solution)/shard_map/ppermute | solution.py:20
  331.9 8.0 %copy-start.14 = (bf16[24,64,512]{2,1,0:T(8,128)(2,1)}, bf16[24,64,512]{2,1,0:T(8,128)(2,1)S(1)}, u32[]{:S(2)}) copy-start(bf16[24,64,512]{2,1,0:T(8,128)(2,1)S(1)} %get-tuple-element.37) | copy-start | bytes 4718596
  331.9 10.0 %copy-start.12 = (bf16[24,64,512]{2,1,0:T(8,128)(2,1)}, bf16[24,64,512]{2,1,0:T(8,128)(2,1)S(1)}, u32[]{:S(2)}) copy-start(bf16[24,64,512]{2,1,0:T(8,128)(2,1)S(1)} %get-tuple-element.36) | copy-start | bytes 4718596
  336.8 2.1 copy-start.10
  336.8 8.2 %copy-start.7 = (bf16[25,66,512]{2,1,0:T(8,128)(2,1)}, bf16[25,66,512]{2,1,0:T(8,128)(2,1)S(1)}, u32[]{:S(2)}) copy-start(bf16[25,66,512]{2,1,0:T(8,128)(2,1)S(1)} %get-tuple-element.29) | copy-start | bytes 5068804
  346.1 3.7 copy-start.16
  349.8 3.0 copy-start.4
  421.7 2.6 copy-start.11
  421.7 3.8 slice-start.2
  424.4 1.2 slice-start.3
  425.6 1.5 copy-start.8
  430.3 1.4 copy-start.15
  431.7 1.4 copy-start.13
  516.4 9.2 %copy-start.17 = (f32[616,512]{1,0:T(8,128)S(1)}, f32[616,512]{1,0:T(8,128)}, u32[]{:S(2)}) copy-start(f32[616,512]{1,0:T(8,128)} %get-tuple-element.13) | copy-start | bytes 3784708
  516.4 10.4 %copy-start.1 = (bf16[616,512]{1,0:T(8,128)(2,1)S(1)}, bf16[616,512]{1,0:T(8,128)(2,1)}, u32[]{:S(2)}) copy-start(bf16[616,512]{1,0:T(8,128)(2,1)} %param.13) | copy-start | bytes 1892356
Sparse Core Ops, SparseCore 0:
  350.0 166.4 all-reduce.2
where the time goes:
time: 542 us; the launch traced here: 534 us
  waiting for transfers between devices  192 us (35%)
  local copies, waits for them, and re-layouts  91 us (17%)
  blocking collectives  86.2 us (16%)
  matrix products  69.9 us (13%)
  other arithmetic  46.6 us (9%)
  starting transfers between devices  33.1 us (6%)
  between operations  15.2 us (3%)
    ppermute x4, waiting for transfers between devices, padded_2(): before = lax.ppermute(last, axis, up)  105 us
    psum x1, waiting for transfers between devices, shards(): lax.psum((conv_part, encoder_part, gain_part), ('lat', 'lon'))  79.2 us
    psum x1, blocking collectives, shards(): lax.psum((conv_part, encoder_part, gain_part), ('lat', 'lon'))  66 us
    gather x3, local copies, waits for them, and re-layouts, shards(): jnp.take(spectra.reshape(blocks, block_rows, channels), source_block, axi...  38 us
    all_gather x1, blocking collectives, gather_turned(): lax.all_gather(both, axis, axis=0, tiled=True)  20.2 us
    reshape x1, local copies, waits for them, and re-layouts, shards(): slot_spectra = arrived.reshape(slots * block_rows, channels)  20.1 us
    ppermute x4, starting transfers between devices, padded_2(): after = lax.ppermute(leading, axis, down)  18.6 us
    dot_general x9, matrix products, shards(): lax.dot_general(back_window, conv_weight[row_shift, col_shift], (((1,), (...  12.3 us
  transfers between devices with their start and end apart: 10, of which 5 were waited for; matrix products, arithmetic and copies ran while one was open for 12% of the time, Pallas kernels for 0%

commit v1 on v0

--- a/solution.py
+++ b/solution.py
@@ -7,6 +7,11 @@
 PH = 8
 PW = 16
 MOST = 3
+
+
+def exchange_gather(array, axis, dim):
+    repeated = jnp.stack([array] * lax.axis_size(axis))
+    return jnp.concatenate(lax.all_to_all(repeated, axis, 0, 0), axis=dim)
 
 
 def padded_2(shard, sides, width, wrap):
@@ -25,7 +30,7 @@
 def gather_turned(arrays, axis, dims):
     turned = [jnp.moveaxis(a, dim, 0) for a, dim in zip(arrays, dims)]
     both = jnp.concatenate([t.reshape(len(t), -1) for t in turned], axis=1)
-    result, at, finished = (lax.all_gather(both, axis, axis=0, tiled=True), 0, [])
+    result, at, finished = (exchange_gather(both, axis, 0), 0, [])
     for t, dim in zip(turned, dims):
         piece = result[:, at : at + t[0].size].reshape(-1, *t.shape[1:])
         finished.append(jnp.moveaxis(piece, 0, dim))

time: 542 us -> 586 us (1.081)
  waiting for transfers between devices: 192 us -> 219 us
  starting transfers between devices: 33.1 us -> 43.1 us
    psum x1, blocking collectives: 66 us -> 89.7 us  [shards(): lax.psum((conv_part, encoder_part, gain_part), ('lat', 'lon'))]
    all_to_all x1, waiting for transfers between devices: 0.01 us -> 23.5 us  [shards(): lax.all_to_all(taken.reshape(lon_count, MOST, -1), 'lon', split_axis=0, c...]
    all_gather x1 -> x0, blocking collectives: 20.2 us -> none  [gather_turned(): lax.all_gather(both, axis, axis=0, tiled=True)]
    all_to_all x0 -> x1, starting transfers between devices: none -> 8.59 us  [exchange_gather(): return jnp.concatenate(lax.all_to_all(repeated, axis, 0, 0), axis=dim)]
  transfers between devices with their start and end apart: 10 -> 11, of which waited for: 5 -> 6; matrix products, arithmetic and copies ran while one was open for 12% -> 13% of each run, Pallas kernels for 0% -> 0%
where the time goes in v1:
time: 586 us; the launch traced here: 578 us
  waiting for transfers between devices  219 us (37%)
  local copies, waits for them, and re-layouts  92.4 us (16%)
  blocking collectives  89.7 us (15%)
  matrix products  71.5 us (12%)
  other arithmetic  46.6 us (8%)
  starting transfers between devices  43.1 us (7%)
  between operations  15.2 us (3%)
    ppermute x4, waiting for transfers between devices, padded_2(): before = lax.ppermute(last, axis, up)  109 us
    psum x1, blocking collectives, shards(): lax.psum((conv_part, encoder_part, gain_part), ('lat', 'lon'))  89.7 us
    psum x1, waiting for transfers between devices, shards(): lax.psum((conv_part, encoder_part, gain_part), ('lat', 'lon'))  79.3 us
    gather x3, local copies, waits for them, and re-layouts, shards(): jnp.take(spectra.reshape(blocks, block_rows, channels), source_block, axi...  38 us
    all_to_all x1, waiting for transfers between devices, shards(): lax.all_to_all(taken.reshape(lon_count, MOST, -1), 'lon', split_axis=0, c...  23.5 us
    reshape x1, local copies, waits for them, and re-layouts, shards(): slot_spectra = arrived.reshape(slots * block_rows, channels)  20.1 us
    ppermute x4, starting transfers between devices, padded_2(): after = lax.ppermute(leading, axis, down)  15.2 us
    dot_general x9, matrix products, shards(): lax.dot_general(back_window, conv_weight[row_shift, col_shift], (((1,), (...  13.8 us
  transfers between devices with their start and end apart: 11, of which 6 were waited for; matrix products, arithmetic and copies ran while one was open for 13% of the time, Pallas kernels for 0%

profile of v1, /device:TPU:1, one launch (start us, length us, event | category | flops | bytes accessed | tf_op | source)
XLA Modules:
  0.0 577.5 jit_solution(634173661317245751)
XLA Ops:
  8.6 8.6 %all-to-all-start = ((s32[16,24,3]{1,2,0:T(4,128)}), s32[16,24,3]{1,2,0:T(4,128)S(1)}, u32[]{:S(2)}, u32[]{:S(2)}) async-start(s32[16,24,3]{1,2,0:T(4,128)} %stack.22), calls=%async_computation | async-start | bytes 65536 | tf_op jit(solution)/shard_map/all_to_all | solution.py:14
  19.7 4.6 copy_bitcast_fusion
  26.4 7.6 %gather_fusion = bf16[48,128,616]{1,2,0:T(8,128)(2,1)} fusion(bf16[24,128,616]{1,2,0:T(8,128)(2,1)} %copy_bitcast_fusion, s32[1024]{0:T(1024)S(1)} %get-tuple-element.49), kind=kCustom, calls=%fused_computation | custom fusion | bytes 15139008 | tf_op jit(solution)/shard_map/jit(_take)/gather | solution.py:114
  33.9 10.3 %copy.100 = bf16[48,128,616]{2,1,0:T(8,128)(2,1)} copy(bf16[48,128,616]{1,2,0:T(8,128)(2,1)} %gather_fusion) | data formatting | bytes 15138816 | tf_op jit(solution)/shard_map/jit(_take)/gather | solution.py:114
  44.2 20.1 %gather.11 = bf16[16,3,78848]{2,1,0:T(4,128)(2,1)} reshape(bf16[48,128,616]{2,1,0:T(8,128)(2,1)} %copy.100) | data formatting | bytes 15138816 | tf_op jit(solution)/shard_map/jit(_take)/gather | solution.py:114
  64.3 9.7 %select_select_fusion = bf16[16,3,78848]{2,1,0:T(4,128)(2,1)} fusion(bf16[16,3,78848]{2,1,0:T(4,128)(2,1)} %gather.11, pred[16,3]{1,0:T(8,128)(4,1)S(1)} %copy.98, pred[16,3]{1,0:T(8,128)(4,1)S(1)} %broadcast_in_dim.57), kind=kLoop, calls=%fused_computation.9 | loop fusion | flops 7569408 | bytes 15138912 | tf_op jit(solution)/shard_map/jit(_where)/select_n | solution.py:115
  74.0 6.9 %all-to-all-start.1 = ((bf16[16,3,78848]{2,1,0:T(4,128)(2,1)}), bf16[16,3,78848]{2,1,0:T(4,128)(2,1)}, u32[]{:S(2)}, u32[]{:S(2)}) async-start(bf16[16,3,78848]{2,1,0:T(4,128)(2,1)} %select_select_fusion), calls=%async_computation.1 | async-start | bytes 20185088 | tf_op jit(solution)/shard_map/all_to_all | solution.py:116
  81.1 1.4 collective-permute-start.4
  82.4 3.5 collective-permute-start.5
  85.9 3.8 fusion.41
  90.6 1.6 copy.114
  92.2 108.9 %collective-permute-done.4 = bf16[24,1,512]{2,1,0:T(2,128)(2,1)S(1)} collective-permute-done((bf16[24,1,512]{2,1,0:T(2,128)(2,1)S(1)}, bf16[24,1,512]{2,1,0:T(2,128)(2,1)S(1)}, u32[]{:S(2)}, u32[]{:S(2)}) %collective-permute-start.4) | collective-permute-done | bytes 24608 | tf_op jit(solution)/shard_map/ppermute | solution.py:24
  201.1 4.6 collective-permute-done.5
  205.7 5.0 collective-permute-start.6
  210.8 3.5 collective-permute-start.7
  214.3 1.1 pad_maximum_fusion.2
  215.5 2.0 pad_maximum_fusion.1
  217.5 2.3 fusion.96
  219.9 1.0 fusion.49
  222.0 1.1 convolution_add_fusion.5
  223.1 1.0 convolution_add_fusion.4
  225.0 1.1 fusion.10
  226.1 1.0 fusion.9
  227.1 1.0 convolution_add_fusion.1
  228.1 2.7 convolution_add_fusion
  230.9 23.5 %all-to-all-done.1 = bf16[16,3,78848]{2,1,0:T(4,128)(2,1)} async-done(((bf16[16,3,78848]{2,1,0:T(4,128)(2,1)}), bf16[16,3,78848]{2,1,0:T(4,128)(2,1)}, u32[]{:S(2)}, u32[]{:S(2)}) %all-to-all-start.1) | async-done | bytes 7569440 | tf_op jit(solution)/shard_map/all_to_all | solution.py:116
  254.4 20.1 %reshape.273 = bf16[6144,616]{1,0:T(8,128)(2,1)} reshape(bf16[16,3,78848]{2,1,0:T(4,128)(2,1)} %all-to-all-done.1) | data formatting | bytes 15138816 | tf_op jit(solution)/shard_map/reshape | solution.py:119
  274.5 11.7 %multiply_convert_fusion = (bf16[6144,512]{1,0:T(8,128)(2,1)S(1)}, f32[6144,512]{1,0:T(8,128)}) fusion(bf16[6144,616]{1,0:T(8,128)(2,1)} %reshape.273, bf16[616,512]{1,0:T(8,128)(2,1)S(1)} %copy-done), kind=kOutput, calls=%fused_computation.7 | convolution fusion | flops 3891265536 | bytes 27074560 | tf_op jit(solution)/shard_map/dot_general | solution.py:120
  286.3 1.8 fusion.101
  288.1 12.0 %fusion.1 = f32[12,128,512]{2,0,1:T(8,128)S(1)} fusion(f32[48,128,512]{2,1,0:T(8,128)S(1)} %fusion.101, s32[48]{0:T(128)S(1)} %eq.86), kind=kOutput, calls=%fused_computation.5 | convolution fusion | flops 452985408 | bytes 15728832 | tf_op jit(solution)/shard_map/sq,spd->qpd/dot_general | solution.py:135
  300.1 1.8 copy.103
  302.0 2.0 copy.104
  305.6 2.2 fusion.13
  307.9 2.2 multiply_convert_fusion.2
  310.2 1.1 copy-done.5
  311.5 4.8 collective-permute-start.1
  316.2 6.6 %gather_fusion.1 = bf16[48,128,512]{2,1,0:T(8,128)(2,1)} fusion(bf16[12,128,512]{2,1,0:T(8,128)(2,1)} %bitcast.197, s32[1024]{0:T(1024)S(1)} %get-tuple-element.48), kind=kCustom, calls=%fused_computation.1 | custom fusion | bytes 12583104 | tf_op jit(solution)/shard_map/jit(_take)/gather | solution.py:180
  322.8 5.3 fusion.6
  328.1 7.8 %fusion = bf16[6144,512]{1,0:T(8,128)(2,1)S(1)} fusion(f32[6144,512]{1,0:T(8,128)} %get-tuple-element.47, bf16[48,128,512]{2,1,0:T(8,128)(2,1)S(1)} %fusion.6), kind=kLoop, calls=%fused_computation.4 | loop fusion | flops 31457280 | bytes 25165824 | tf_op jit(solution)/shard_map/convert_element_type | solution.py:184
  335.9 5.1 fusion.102
  341.1 7.4 %collective-permute-start.2 = (bf16[1,66,512]{2,1,0:T(8,128)(2,1)S(1)}, bf16[1,66,512]{2,1,0:T(8,128)(2,1)S(1)}, u32[]{:S(2)}, u32[]{:S(2)}) collective-permute-start(bf16[1,66,512]{2,1,0:T(8,128)(2,1)S(1)} %get-tuple-element.30), channel_id=1, source_target_pairs={{0,16},{16,32},{32,48},{48,64},{64,80},{80,96},{96,112},{1,17},{17... | collective-permute-start | bytes 202760 | tf_op jit(solution)/shard_map/ppermute | solution.py:24
  348.5 1.9 collective-permute-start.3
  350.4 1.1 pad_maximum_fusion.4
  351.6 2.6 collective-permute-done.3
  354.2 2.3 maximum_maximum_fusion
  357.5 1.0 fusion.26
  358.6 1.0 fusion.25
  362.6 1.0 fusion.21
  363.6 1.0 fusion.20
  364.7 1.0 fusion.19
  365.7 3.7 copy-done.17
  369.6 2.9 copy.106
  372.5 2.3 fusion.15
  374.7 89.7 %psum.23 = f32[512]{0:T(512)S(1)} all-reduce(f32[512]{0:T(512)S(1)} %fusion.15), channel_id=1, replica_groups=mesh['lat'=8,'lon'=16] {'lat','lon'}, use_global_device_ids=true, to_apply=%region_14.15 | all-reduce | flops 512 | bytes 4096 | tf_op jit(solution)/shard_map/psum | solution.py:190
  465.0 2.6 fusion.43
  467.7 1.1 fusion.95
  470.4 1.1 fusion.94
  472.5 1.1 convolution_add_fusion.11
  473.6 1.1 convolution_add_fusion.10
  475.0 1.1 fusion.12
  478.4 2.2 fusion.17
  480.5 79.3 %all-reduce.3.cloned.1.call-done = (f32[3,3,512,512]{3,2,1,0:T(8,128)}, f32[616,512]{1,0:T(8,128)}) async-done(((f32[3,3,512,512]{3,2,1,0:T(8,128)}, f32[616,512]{1,0:T(8,128)}), (f32[3,3,512,512]{3,2,1,0:T(8,128)}, f32[616,512]{1,0:T(8,128)})) %all-reduce.3.cloned.1.call-update) | async-done | bytes 10698768 | tf_op jit(solution)/shard_map/psum | solution.py:190
  559.8 9.2 %broadcast_multiply_fusion = f32[3,3,512,512]{3,2,1,0:T(8,128)} fusion(f32[3,3,512,512]{3,2,1,0:T(8,128)} %get-tuple-element.12), kind=kLoop, calls=%fused_computation.14 | loop fusion | flops 2359296 | bytes 18874368 | tf_op jit(solution)/shard_map/mul | solution.py:193
  569.0 1.2 broadcast_multiply_fusion.1
  (119 shorter events, 20.9 us)
Async XLA Ops:
  7.2 267.4 %copy-start = (bf16[616,512]{1,0:T(8,128)(2,1)S(1)}, bf16[616,512]{1,0:T(8,128)(2,1)}, u32[]{:S(2)}) copy-start(bf16[616,512]{1,0:T(8,128)(2,1)} %param.13) | copy-start | bytes 1892356
  8.6 16.0 %all-to-all-start = ((s32[16,24,3]{1,2,0:T(4,128)}), s32[16,24,3]{1,2,0:T(4,128)S(1)}, u32[]{:S(2)}, u32[]{:S(2)}) async-start(s32[16,24,3]{1,2,0:T(4,128)} %stack.22), calls=%async_computation | async-start | bytes 65536 | tf_op jit(solution)/shard_map/all_to_all | solution.py:14
  74.0 6.9 %copy-start.2 = (bf16[24,64,512]{2,1,0:T(8,128)(2,1)S(1)}, bf16[24,64,512]{2,1,0:T(8,128)(2,1)}, u32[]{:S(2)}) copy-start(bf16[24,64,512]{2,1,0:T(8,128)(2,1)} %param.17) | copy-start | bytes 4718596
  74.0 180.4 %all-to-all-start.1 = ((bf16[16,3,78848]{2,1,0:T(4,128)(2,1)}), bf16[16,3,78848]{2,1,0:T(4,128)(2,1)}, u32[]{:S(2)}, u32[]{:S(2)}) async-start(bf16[16,3,78848]{2,1,0:T(4,128)(2,1)} %select_select_fusion), calls=%async_computation.1 | async-start | bytes 20185088 | tf_op jit(solution)/shard_map/all_to_all | solution.py:116
  80.9 478.9 %all-reduce.3.cloned.1.call-start = ((), (), s32[]{:S(2)}) async-start(), calls=%async_computation.2 | async-start | bytes 21397504 | tf_op jit(solution)/shard_map/psum | solution.py:190
  81.1 120.0 %collective-permute-start.4 = (bf16[24,1,512]{2,1,0:T(2,128)(2,1)S(1)}, bf16[24,1,512]{2,1,0:T(2,128)(2,1)S(1)}, u32[]{:S(2)}, u32[]{:S(2)}) collective-permute-start(bf16[24,1,512]{2,1,0:T(2,128)(2,1)S(1)} %get-tuple-element.42), channel_id=1, source_target_pairs={{0,1},{1,2},{2,3},{3,4},{4,5},{5,6},{6,7},{7,8},{8,9},{9,10},{10,1... | collective-permute-start | bytes 73736 | tf_op jit(solution)/shard_map/ppermute | solution.py:24
  82.4 123.2 %collective-permute-start.5 = (bf16[24,1,512]{2,1,0:T(2,128)(2,1)S(1)}, bf16[24,1,512]{2,1,0:T(2,128)(2,1)S(1)}, u32[]{:S(2)}, u32[]{:S(2)}) collective-permute-start(bf16[24,1,512]{2,1,0:T(2,128)(2,1)S(1)} %get-tuple-element.43), channel_id=1, source_target_pairs={{1,0},{2,1},{3,2},{4,3},{5,4},{6,5},{7,6},{8,7},{9,8},{10,9},{11,1... | collective-permute-start | bytes 73736 | tf_op jit(solution)/shard_map/ppermute | solution.py:25
  85.9 4.1 copy-start.19
  205.7 9.7 %collective-permute-start.6 = (bf16[1,66,512]{2,1,0:T(8,128)(2,1)S(1)}, bf16[1,66,512]{2,1,0:T(8,128)(2,1)S(1)}, u32[]{:S(2)}, u32[]{:S(2)}) collective-permute-start(bf16[1,66,512]{2,1,0:T(8,128)(2,1)S(1)} %get-tuple-element.34), channel_id=1, source_target_pairs={{16,0},{32,16},{48,32},{64,48},{80,64},{96,80},{112,96},{17,1},{33... | collective-permute-start | bytes 202760 | tf_op jit(solution)/shard_map/ppermute | solution.py:25
  210.8 4.7 collective-permute-start.7
  215.5 4.4 slice-start
  217.5 2.4 slice-start.1
  223.1 1.9 copy-start.9
  274.5 11.7 %copy-start.10 = (bf16[6,8,128,128]{3,2,1,0:T(8,128)(2,1)S(1)}, bf16[6,8,128,128]{3,2,1,0:T(8,128)(2,1)}, u32[]{:S(2)}) copy-start(bf16[6,8,128,128]{3,2,1,0:T(8,128)(2,1)} %copy.114) | copy-start | bytes 4718596
  302.0 3.0 copy-start.3
  302.0 3.0 copy-start.20
  310.2 1.1 copy-start.5
  311.4 29.6 %collective-permute-start = (bf16[24,1,512]{2,1,0:T(2,128)(2,1)S(1)}, bf16[24,1,512]{2,1,0:T(2,128)(2,1)S(1)}, u32[]{:S(2)}, u32[]{:S(2)}) collective-permute-start(bf16[24,1,512]{2,1,0:T(2,128)(2,1)S(1)} %get-tuple-element.38), channel_id=1, source_target_pairs={{0,1},{1,2},{2,3},{3,4},{4,5},{5,6},{6,7},{7,8},{8,9},{9,10},{10,1... | collective-permute-start | bytes 73736 | tf_op jit(solution)/shard_map/ppermute | solution.py:24
  311.5 29.6 %collective-permute-start.1 = (bf16[24,1,512]{2,1,0:T(2,128)(2,1)S(1)}, bf16[24,1,512]{2,1,0:T(2,128)(2,1)S(1)}, u32[]{:S(2)}, u32[]{:S(2)}) collective-permute-start(bf16[24,1,512]{2,1,0:T(2,128)(2,1)S(1)} %get-tuple-element.39), channel_id=1, source_target_pairs={{1,0},{2,1},{3,2},{4,3},{5,4},{6,5},{7,6},{8,7},{9,8},{10,9},{11,1... | collective-permute-start | bytes 73736 | tf_op jit(solution)/shard_map/ppermute | solution.py:25
  322.8 13.0 %slice-start.4 = ((s8[7864320]{0:T(1024)(128)(4,1)}), s8[4194304]{0:T(1024)(128)(4,1)S(1)}, s32[]{:S(2)}) async-start(s8[7864320]{0:T(1024)(128)(4,1)} %bitcast.214), calls=%async_computation.7 | async-start | bytes 8388608
  328.1 7.8 %slice-start.5 = ((s8[7864320]{0:T(1024)(128)(4,1)}), s8[3670016]{0:T(1024)(128)(4,1)S(1)}, s32[]{:S(2)}) async-start(s8[7864320]{0:T(1024)(128)(4,1)} %bitcast.214), calls=%async_computation.8 | async-start | bytes 7340032
  335.9 5.2 copy-start.6
  341.1 10.5 %collective-permute-start.2 = (bf16[1,66,512]{2,1,0:T(8,128)(2,1)S(1)}, bf16[1,66,512]{2,1,0:T(8,128)(2,1)S(1)}, u32[]{:S(2)}, u32[]{:S(2)}) collective-permute-start(bf16[1,66,512]{2,1,0:T(8,128)(2,1)S(1)} %get-tuple-element.30), channel_id=1, source_target_pairs={{0,16},{16,32},{32,48},{48,64},{64,80},{80,96},{96,112},{1,17},{17... | collective-permute-start | bytes 202760 | tf_op jit(solution)/shard_map/ppermute | solution.py:24
  348.5 5.7 collective-permute-start.3
  351.6 8.0 %copy-start.15 = (bf16[24,64,512]{2,1,0:T(8,128)(2,1)}, bf16[24,64,512]{2,1,0:T(8,128)(2,1)S(1)}, u32[]{:S(2)}) copy-start(bf16[24,64,512]{2,1,0:T(8,128)(2,1)S(1)} %get-tuple-element.37) | copy-start | bytes 4718596
  351.6 10.0 %copy-start.13 = (bf16[24,64,512]{2,1,0:T(8,128)(2,1)}, bf16[24,64,512]{2,1,0:T(8,128)(2,1)S(1)}, u32[]{:S(2)}) copy-start(bf16[24,64,512]{2,1,0:T(8,128)(2,1)S(1)} %get-tuple-element.36) | copy-start | bytes 4718596
  356.5 2.1 copy-start.11
  356.5 8.2 %copy-start.7 = (bf16[25,66,512]{2,1,0:T(8,128)(2,1)}, bf16[25,66,512]{2,1,0:T(8,128)(2,1)S(1)}, u32[]{:S(2)}) copy-start(bf16[25,66,512]{2,1,0:T(8,128)(2,1)S(1)} %get-tuple-element.29) | copy-start | bytes 5068804
  365.7 3.7 copy-start.17
  369.5 3.0 copy-start.4
  465.0 2.6 copy-start.12
  465.0 3.8 slice-start.2
  467.7 1.2 slice-start.3
  468.9 1.5 copy-start.8
  473.6 1.4 copy-start.16
  475.0 1.4 copy-start.14
  559.8 9.2 %copy-start.18 = (f32[616,512]{1,0:T(8,128)S(1)}, f32[616,512]{1,0:T(8,128)}, u32[]{:S(2)}) copy-start(f32[616,512]{1,0:T(8,128)} %get-tuple-element.13) | copy-start | bytes 3784708
  559.8 10.4 %copy-start.1 = (bf16[616,512]{1,0:T(8,128)(2,1)S(1)}, bf16[616,512]{1,0:T(8,128)(2,1)}, u32[]{:S(2)}) copy-start(bf16[616,512]{1,0:T(8,128)(2,1)} %param.13) | copy-start | bytes 1892356
Sparse Core Ops, SparseCore 0:
  369.6 190.1 all-reduce.2
